TPU v7x, 256 devices: a 4x2x16 block of a 4x16x16 slice. The times are simulated.
256 devices in a mesh: groups: 2 (over y), dp: 32 (over z, core), mp: 4 (over x).
Axes of the slice: x: 4, y: 2, z: 16, core: 2. Of those that a mesh axis runs over, the one named last changes fastest.
The devices are a block of a 4x16x16 slice.
Arguments:
- tokens: bfloat16 [8192, 7168], P(('groups', 'dp')), parts along dimension 0, may hold values from -20 to 20, as said below
- w_down: bfloat16 [7168, 1536], P('dp', 'mp'), may hold values from -3 to 3, as said below
- gain: float32 [1536], P('mp'), may hold values from 0.25 to 1.75
- w_up: bfloat16 [1536, 26112], P('dp', 'mp'), may hold values from -0.15625 to 0.15625
- head_counts: int32 [4], replicated, may hold values from 30 to 34, as said below
- cotangent: bfloat16 [8192, 26112], P(('groups', 'dp'), 'mp'), parts along dimension 0, may hold values from -6 to 6
Outputs:
- queries: bfloat16 [8192, 26112], P(('groups', 'dp'), 'mp'), parts along dimension 0
- grad_tokens: bfloat16 [8192, 7168], P(('groups', 'dp'), 'mp'), parts along dimension 0
There are 2 independent parts, one for each index of `groups`. A program takes and returns all parts, laid end to end along the dimension named above; an argument that names none is the same for every part. Nothing has to cross between parts.
Inputs may be any that keep to these rules, and one draw needn't show every extreme that they name: `tokens`: hidden states of order one with token scales that differ. `w_down`: entries of order 7168^(-1/2). `head_counts`: the entries sum to 128; one of them is 34.
All inputs are finite; a program needn't handle non-finite values.
Results may differ from a plain program's by a relative error of at most 0.018.
Values may be sent and summed in bfloat16 or wider, within the bound.
A program may use at most 128 MiB of HBM per device.

v0:
```python
import jax
import jax.numpy as jnp
from jax import lax
from jax.sharding import PartitionSpec as P

HD = 192


def laid_out(blocks, dim):
    shape = list(blocks.shape[1:])
    shape[dim] *= blocks.shape[0]
    return jnp.moveaxis(blocks, 0, dim).reshape(shape)


def from_everyone(array, axis):
    size = lax.axis_size(axis)
    return lax.all_to_all(
        jnp.broadcast_to(array[None], (size, *array.shape)), axis, 0, 0, tiled=True
    )


def gather_directly(array, axis, dim):
    return laid_out(from_everyone(array, axis), dim)


def cut_along(array, dim, size):
    shape = array.shape
    blocks = array.reshape(*shape[:dim], size, shape[dim] // size, *shape[dim + 1 :])
    return jnp.moveaxis(blocks, dim, 0)


def sent_and_summed(array, axis, dim):
    size = lax.axis_size(axis)
    blocks = lax.all_to_all(cut_along(array, dim, size), axis, 0, 0, tiled=True)
    return jnp.sum(blocks.astype(jnp.float32), axis=0)


def contract_last(left, right):
    return lax.dot_general(
        left, right, (((1,), (1,)), ((), ())), preferred_element_type=jnp.float32
    )


def body(tokens, w_down, gain, w_up, head_counts, cotangent):
    block_cols = w_up.shape[1]
    latent_width = w_down.shape[1] * lax.axis_size("mp")
    position = lax.axis_index("mp")
    held_heads = lax.dynamic_slice_in_dim(head_counts, position, 1, 0)
    slot_index = jnp.arange(block_cols, dtype=jnp.int32) // HD
    keep_mask = (slot_index < held_heads).astype(jnp.float32)
    down_whole = lax.all_gather(w_down, "dp", axis=0, tiled=True)
    latent_raw = jnp.dot(tokens, down_whole, preferred_element_type=jnp.float32)
    squares = lax.psum(jnp.sum(latent_raw * latent_raw, axis=1, keepdims=True), "mp")
    root_mean = jnp.sqrt(squares / latent_width + 1e-06)
    latent_local = (latent_raw / root_mean * gain).astype(jnp.bfloat16)
    latent = gather_directly(latent_local, "mp", 1)
    masked = cotangent * keep_mask.astype(jnp.bfloat16)
    up_whole = lax.all_gather(w_up, "dp", axis=0, tiled=True)
    query_total = jnp.dot(latent, up_whole, preferred_element_type=jnp.float32)
    grad_partial = contract_last(masked, up_whole)
    queries = (query_total * keep_mask).astype(jnp.bfloat16)
    grad_latent = sent_and_summed(grad_partial.astype(jnp.bfloat16), "mp", 1)
    inner_dot = lax.psum(jnp.sum(gain * grad_latent * latent_raw, axis=1, keepdims=True), "mp")
    grad_raw = (
        gain * grad_latent / root_mean - latent_raw * inner_dot / (latent_width * root_mean**3)
    ).astype(jnp.bfloat16)
    partial_value = contract_last(grad_raw, down_whole).astype(jnp.bfloat16).astype(jnp.float32)
    grad_tokens = sent_and_summed(partial_value.astype(jnp.bfloat16), "mp", 1).astype(jnp.bfloat16)
    return (queries, grad_tokens)


def solution(mesh):
    in_specs = (
        P(("groups", "dp"), None),
        P("dp", "mp"),
        P("mp"),
        P("dp", "mp"),
        P(),
        P(("groups", "dp"), "mp"),
    )
    out_specs = (P(("groups", "dp"), "mp"), P(("groups", "dp"), "mp"))
    return jax.shard_map(body, mesh=mesh, in_specs=in_specs, out_specs=out_specs, check_vma=False)
```

profile of v0, /device:TPU:40, one launch (start us, length us, event | category | flops | bytes accessed | tf_op | source)
XLA Modules:
  0.0 279.0 jit_solution(305809374449515332)
XLA Ops:
  7.2 0.0 copy-start
  7.2 0.1 all-gather.5.cloned.1.call-start
  7.3 0.7 all-gather.5.cloned.1.call-update
  8.0 0.1 all-gather.3.cloned.1.call-start
  8.1 0.7 all-gather.3.cloned.1.call-update
  8.8 1.2 dynamic_slice.3
  10.0 0.7 fusion.12
  10.7 0.0 copy-start.1
  10.7 133.8 %all-gather.5.cloned.1.call-done = bf16[1536,6528]{1,0:T(8,128)(2,1)} async-done(((bf16[48,6528]{1,0:T(8,128)(2,1)}), bf16[1536,6528]{1,0:T(8,128)(2,1)}) %all-gather.5.cloned.1.call-update) | async-done | bytes 20054032 | tf_op jit(solution)/shard_map/all_gather | solution.py:58
  144.5 10.2 %convolution_convert_fusion.1 = bf16[128,1536]{1,0:T(8,128)(2,1)S(1)} fusion(bf16[1536,6528]{1,0:T(8,128)(2,1)} %all-gather.5.cloned.1.call-done, bf16[128,6528]{1,0:T(8,128)(2,1)} %param.11, bf16[6528]{0:T(1024)(128)(2,1)S(1)} %fusion.12), kind=kOutput, calls=%fused_computation.3 | convolution fusion | flops 2567946240 | bytes 22131456 | tf_op jit(solution)/shard_map/dot_general | solution.py:39
  154.7 12.5 %all_to_all.15 = bf16[4,128,384]{2,1,0:T(8,128)(2,1)S(1)} all-to-all(bf16[4,128,384]{2,1,0:T(8,128)(2,1)S(1)} %bitcast.33), channel_id=1, replica_groups=mesh['groups'=2,'dp'=32,'mp'=4] {'mp'}, dimensions={0} | all-to-all | bytes 786432 | tf_op jit(solution)/shard_map/all_to_all | solution.py:34
  167.3 50.5 %all-gather.3.cloned.1.call-done = bf16[7168,384]{1,0:T(8,128)(2,1)} async-done(((bf16[224,384]{1,0:T(8,128)(2,1)}), bf16[7168,384]{1,0:T(8,128)(2,1)}) %all-gather.3.cloned.1.call-update) | async-done | bytes 5505040 | tf_op jit(solution)/shard_map/all_gather | solution.py:51
  217.8 0.0 copy-done
  217.8 0.0 copy-done.1
  217.9 3.8 %multiply_reduce_fusion = (f32[128]{0:T(128)S(1)}, f32[128]{0:T(128)S(1)}, f32[128,384]{1,0:T(8,128)S(1)}) fusion(f32[128,384]{1,0:T(8,128)S(1)} %convert_reduce_fusion, f32[384]{0:T(512)S(1)} %copy-done.1, bf16[128,7168]{1,0:T(8,128)(2,1)S(1)} %copy-done, bf16[7168,384]{1,0:T(8,128)(2,1)} %all-gather.3.cloned.1.call-done), kind=kOutput, calls=%fused_computation.10 | convolution fusion | flops 704888576 | bytes 7735808 | tf_op jit(solution)/shard_map/dot_general | solution.py:52
  221.6 10.5 %all-reduce = (f32[128,1]{0,1:T(1,128)S(1)}, f32[128]{0:T(128)S(1)}) all-reduce(f32[128,1]{0,1:T(1,128)S(1)} %bitcast.34, f32[128]{0:T(128)S(1)} %get-tuple-element.2), channel_id=1, replica_groups=mesh['groups'=2,'dp'=32,'mp'=4] {'mp'}, use_global_device_ids=true, to_apply=%region_1.2 | all-reduce | flops 256 | bytes 2048 | tf_op jit(solution)/shard_map/psum | solution.py:53
  232.1 0.1 multiply_convert_fusion
  232.2 0.1 copy.9
  232.3 0.8 broadcast_in_dim.7
  233.1 3.6 %all-to-all-start = ((bf16[4,128,384]{1,2,0:T(8,128)(2,1)}), bf16[4,128,384]{1,2,0:T(8,128)(2,1)S(1)}, u32[]{:S(2)}, u32[]{:S(2)}) async-start(bf16[4,128,384]{1,2,0:T(8,128)(2,1)} %broadcast_in_dim.7), calls=%async_computation | async-start | bytes 786432 | tf_op jit(solution)/shard_map/all_to_all | solution.py:17
  236.7 4.4 %convolution_convert_fusion = bf16[128,7168]{1,0:T(8,128)(2,1)S(1)} fusion(bf16[7168,384]{1,0:T(8,128)(2,1)} %all-gather.3.cloned.1.call-done, f32[128,384]{1,0:T(8,128)S(1)} %get-tuple-element.8, f32[128,384]{1,0:T(8,128)S(1)} %convert_reduce_fusion, f32[128]{0:T(128)S(1)} %get-tuple-element.6, f32[128]{0:T(128)S(1)} %get-tuple-element.5, ...), kind=kOutput, calls=%fused_computation.2 | convolution fusion | flops 705855488 | bytes 7736320 | tf_op jit(solution)/shard_map/dot_general | solution.py:39
  241.1 1.4 copy.16
  242.5 1.5 all-to-all-done
  244.0 4.5 %all-to-all-start.2 = ((bf16[4,128,1792]{2,1,0:T(8,128)(2,1)}), bf16[4,128,1792]{2,1,0:T(8,128)(2,1)}, u32[]{:S(2)}, u32[]{:S(2)}) async-start(bf16[4,128,1792]{2,1,0:T(8,128)(2,1)} %bitcast.29), calls=%async_computation.2 | async-start | bytes 3670016 | tf_op jit(solution)/shard_map/all_to_all | solution.py:34
  248.5 0.7 fusion.10
  249.1 10.9 %fusion = bf16[128,6528]{1,0:T(8,128)(2,1)} fusion(bf16[128,1536]{0,1:T(8,128)(2,1)S(1)} %bitcast.31, bf16[1536,6528]{1,0:T(8,128)(2,1)} %all-gather.5.cloned.1.call-done, f32[6528]{0:T(1024)S(1)} %fusion.10), kind=kOutput, calls=%fused_computation.1 | convolution fusion | flops 2568585216 | bytes 22144512 | tf_op jit(solution)/shard_map/dot_general | solution.py:59
  260.0 9.5 %all-to-all-done.2 = bf16[4,128,1792]{2,1,0:T(8,128)(2,1)} async-done(((bf16[4,128,1792]{2,1,0:T(8,128)(2,1)}), bf16[4,128,1792]{2,1,0:T(8,128)(2,1)}, u32[]{:S(2)}, u32[]{:S(2)}) %all-to-all-start.2) | async-done | bytes 1835040 | tf_op jit(solution)/shard_map/all_to_all | solution.py:34
  269.5 2.7 reduce_sum.42
  (3 shorter events, 0.1 us)
Async XLA Ops:
  7.2 210.7 %copy-start = (bf16[128,7168]{1,0:T(8,128)(2,1)S(1)}, bf16[128,7168]{1,0:T(8,128)(2,1)}, u32[]{:S(2)}) copy-start(bf16[128,7168]{1,0:T(8,128)(2,1)} %param.6) | copy-start | bytes 5505028
  7.2 137.3 %all-gather.5.cloned.1.call-start = ((), (), s32[]{:S(2)}) async-start(), calls=%async_computation.4 | async-start | bytes 20680704 | tf_op jit(solution)/shard_map/all_gather | solution.py:58
  8.0 209.9 %all-gather.3.cloned.1.call-start = ((), (), s32[]{:S(2)}) async-start(), calls=%async_computation.3 | async-start | bytes 5677056 | tf_op jit(solution)/shard_map/all_gather | solution.py:51
  10.7 207.1 %copy-start.1 = (f32[384]{0:T(512)S(1)}, f32[384]{0:T(512)}, u32[]{:S(2)}) copy-start(f32[384]{0:T(512)} %param.8) | copy-start | bytes 4612
  233.1 10.8 %all-to-all-start = ((bf16[4,128,384]{1,2,0:T(8,128)(2,1)}), bf16[4,128,384]{1,2,0:T(8,128)(2,1)S(1)}, u32[]{:S(2)}, u32[]{:S(2)}) async-start(bf16[4,128,384]{1,2,0:T(8,128)(2,1)} %broadcast_in_dim.7), calls=%async_computation | async-start | bytes 786432 | tf_op jit(solution)/shard_map/all_to_all | solution.py:17
  244.0 25.5 %all-to-all-start.2 = ((bf16[4,128,1792]{2,1,0:T(8,128)(2,1)}), bf16[4,128,1792]{2,1,0:T(8,128)(2,1)}, u32[]{:S(2)}, u32[]{:S(2)}) async-start(bf16[4,128,1792]{2,1,0:T(8,128)(2,1)} %bitcast.29), calls=%async_computation.2 | async-start | bytes 3670016 | tf_op jit(solution)/shard_map/all_to_all | solution.py:34
Sparse Core Ops, SparseCore 0:
  9.9 134.5 all-gather.4
  146.3 71.4 all-gather.2
where the time goes:
time: 279 us
  waiting for transfers between devices  197 us (71%)
  matrix products  29.2 us (10%)
  blocking collectives  23 us (8%)
  between operations  14.2 us (5%)
  starting transfers between devices  8.15 us (3%)
  other arithmetic  4.13 us (1%)
  local copies, waits for them, and re-layouts  3.65 us (1%)
    all_gather x1, waiting for transfers between devices, body(): up_whole = lax.all_gather(w_up, 'dp', axis=0, tiled=True)  134 us
    all_gather x1, waiting for transfers between devices, body(): down_whole = lax.all_gather(w_down, 'dp', axis=0, tiled=True)  50.5 us
    dot_general x2, matrix products, contract_last(): lax.dot_general(left, right, (((1,), (1,)), ((), ())), preferred_element_...  14.6 us
    all_to_all x1, blocking collectives, sent_and_summed(): blocks = lax.all_to_all(cut_along(array, dim, size), axis, 0, 0, tiled=True)  12.5 us
    dot_general x1, matrix products, body(): query_total = jnp.dot(latent, up_whole, preferred_element_type=jnp.float32)  10.9 us
    psum x1, blocking collectives, body(): lax.psum(jnp.sum(latent_raw * latent_raw, axis=1, keepdims=True), 'mp')  10.5 us
    all_to_all x1, waiting for transfers between devices, sent_and_summed(): blocks = lax.all_to_all(cut_along(array, dim, size), axis, 0, 0, tiled=True)  9.51 us
  transfers between devices with their start and end apart: 4, of which 4 were waited for; matrix products, arithmetic and copies ran while one was open for 11% of the time, Pallas kernels for 0%

commit v1 on v0

--- a/solution.py
+++ b/solution.py
@@ -48,7 +48,10 @@
     held_heads = lax.dynamic_slice_in_dim(head_counts, position, 1, 0)
     slot_index = jnp.arange(block_cols, dtype=jnp.int32) // HD
     keep_mask = (slot_index < held_heads).astype(jnp.float32)
-    down_whole = lax.all_gather(w_down, "dp", axis=0, tiled=True)
+    count = lax.axis_size("dp")
+    parts = jnp.stack([w_down for _ in range(count)])
+    parts = lax.all_to_all(parts, "dp", split_axis=0, concat_axis=0)
+    down_whole = jnp.concatenate(parts, axis=0)
     latent_raw = jnp.dot(tokens, down_whole, preferred_element_type=jnp.float32)
     squares = lax.psum(jnp.sum(latent_raw * latent_raw, axis=1, keepdims=True), "mp")
     root_mean = jnp.sqrt(squares / latent_width + 1e-06)

time: 279 us -> 485 us (1.74)
  waiting for transfers between devices: 197 us -> 388 us
  starting transfers between devices: 8.15 us -> 18.2 us
    all_to_all x0 -> x1, waiting for transfers between devices: none -> 242 us  [body(): parts = lax.all_to_all(parts, 'dp', split_axis=0, concat_axis=0)]
    all_gather x1 -> x0, waiting for transfers between devices: 50.5 us -> none  [body(): down_whole = lax.all_gather(w_down, 'dp', axis=0, tiled=True)]
    all_to_all x0 -> x1, starting transfers between devices: none -> 10.1 us  [body(): parts = lax.all_to_all(parts, 'dp', split_axis=0, concat_axis=0)]
  transfers between devices with their start and end apart: 4 -> 4, of which waited for: 4 -> 4; matrix products, arithmetic and copies ran while one was open for 11% -> 4% of each run, Pallas kernels for 0% -> 0%
where the time goes in v1:
time: 485 us; the launch traced here: 482 us
  waiting for transfers between devices  388 us (80%)
  matrix products  29.2 us (6%)
  blocking collectives  21.5 us (4%)
  starting transfers between devices  18.2 us (4%)
  between operations  14.2 us (3%)
  local copies, waits for them, and re-layouts  6.59 us (1%)
    all_to_all x1, waiting for transfers between devices, body(): parts = lax.all_to_all(parts, 'dp', split_axis=0, concat_axis=0)  242 us
    all_gather x1, waiting for transfers between devices, body(): up_whole = lax.all_gather(w_up, 'dp', axis=0, tiled=True)  135 us
    dot_general x2, matrix products, contract_last(): lax.dot_general(left, right, (((1,), (1,)), ((), ())), preferred_element_...  14.6 us
    all_to_all x1, blocking collectives, sent_and_summed(): blocks = lax.all_to_all(cut_along(array, dim, size), axis, 0, 0, tiled=True)  12.5 us
    dot_general x1, matrix products, body(): query_total = jnp.dot(latent, up_whole, preferred_element_type=jnp.float32)  10.9 us
    all_to_all x1, starting transfers between devices, body(): parts = lax.all_to_all(parts, 'dp', split_axis=0, concat_axis=0)  10.1 us
  transfers between devices with their start and end apart: 4, of which 4 were waited for; matrix products, arithmetic and copies ran while one was open for 4% of the time, Pallas kernels for 0%

profile of v1, /device:TPU:40, one launch (start us, length us, event | category | flops | bytes accessed | tf_op | source)
XLA Modules:
  0.0 481.7 jit_solution(10771382895924154025)
XLA Ops:
  7.2 0.0 copy-start
  7.2 0.1 all-gather.2.cloned.1.call-start
  7.3 0.7 all-gather.2.cloned.1.call-update
  8.0 1.2 dynamic_slice.3
  9.2 0.7 fusion.12
  9.9 0.0 copy-start.1
  9.9 134.6 %all-gather.2.cloned.1.call-done = bf16[1536,6528]{1,0:T(8,128)(2,1)} async-done(((bf16[48,6528]{1,0:T(8,128)(2,1)}), bf16[1536,6528]{1,0:T(8,128)(2,1)}) %all-gather.2.cloned.1.call-update) | async-done | bytes 20054032 | tf_op jit(solution)/shard_map/all_gather | solution.py:61
  144.5 10.2 %convolution_convert_fusion.1 = bf16[128,1536]{1,0:T(8,128)(2,1)S(1)} fusion(bf16[1536,6528]{1,0:T(8,128)(2,1)} %all-gather.2.cloned.1.call-done, bf16[128,6528]{1,0:T(8,128)(2,1)} %param.11, bf16[6528]{0:T(1024)(128)(2,1)S(1)} %fusion.12), kind=kOutput, calls=%fused_computation.3 | convolution fusion | flops 2567946240 | bytes 22131456 | tf_op jit(solution)/shard_map/dot_general | solution.py:39
  154.7 12.5 %all_to_all.20 = bf16[4,128,384]{2,1,0:T(8,128)(2,1)S(1)} all-to-all(bf16[4,128,384]{2,1,0:T(8,128)(2,1)S(1)} %bitcast.34), channel_id=1, replica_groups=mesh['groups'=2,'dp'=32,'mp'=4] {'mp'}, dimensions={0} | all-to-all | bytes 786432 | tf_op jit(solution)/shard_map/all_to_all | solution.py:34
  167.3 0.0 copy-done.1
  167.3 2.9 stack.2
  170.2 0.0 copy-start.2
  170.2 10.1 %all-to-all-start = ((bf16[32,224,384]{2,1,0:T(8,128)(2,1)}), bf16[32,224,384]{2,1,0:T(8,128)(2,1)}, u32[]{:S(2)}, u32[]{:S(2)}) async-start(bf16[32,224,384]{2,1,0:T(8,128)(2,1)} %stack.2), calls=%async_computation | async-start | bytes 11010048 | tf_op jit(solution)/shard_map/all_to_all | solution.py:53
  180.4 241.9 %all-to-all-done = bf16[32,224,384]{2,1,0:T(8,128)(2,1)} async-done(((bf16[32,224,384]{2,1,0:T(8,128)(2,1)}), bf16[32,224,384]{2,1,0:T(8,128)(2,1)}, u32[]{:S(2)}, u32[]{:S(2)}) %all-to-all-start) | async-done | bytes 5505056 | tf_op jit(solution)/shard_map/all_to_all | solution.py:53
  422.3 0.0 copy-done
  422.3 0.0 copy-done.2
  422.3 3.8 multiply_reduce_fusion
  426.0 8.9 %all-reduce = (f32[128,1]{0,1:T(1,128)S(1)}, f32[128]{0:T(128)S(1)}) all-reduce(f32[128,1]{0,1:T(1,128)S(1)} %bitcast.35, f32[128]{0:T(128)S(1)} %get-tuple-element.2), channel_id=1, replica_groups=mesh['groups'=2,'dp'=32,'mp'=4] {'mp'}, use_global_device_ids=true, to_apply=%region_1.2 | all-reduce | flops 256 | bytes 2048 | tf_op jit(solution)/shard_map/psum | solution.py:56
  435.0 0.1 multiply_convert_fusion
  435.1 0.1 copy.9
  435.2 0.8 broadcast_in_dim.7
  436.0 3.6 all-to-all-start.1
  439.6 4.4 convolution_convert_fusion
  444.0 1.4 copy.16
  445.4 1.5 all-to-all-done.1
  446.9 4.5 all-to-all-start.3
  451.4 0.7 fusion.10
  452.0 10.9 %fusion = bf16[128,6528]{1,0:T(8,128)(2,1)} fusion(bf16[128,1536]{0,1:T(8,128)(2,1)S(1)} %bitcast.32, bf16[1536,6528]{1,0:T(8,128)(2,1)} %all-gather.2.cloned.1.call-done, f32[6528]{0:T(1024)S(1)} %fusion.10), kind=kOutput, calls=%fused_computation.1 | convolution fusion | flops 2568585216 | bytes 22144512 | tf_op jit(solution)/shard_map/dot_general | solution.py:62
  462.9 9.3 %all-to-all-done.3 = bf16[4,128,1792]{2,1,0:T(8,128)(2,1)} async-done(((bf16[4,128,1792]{2,1,0:T(8,128)(2,1)}), bf16[4,128,1792]{2,1,0:T(8,128)(2,1)}, u32[]{:S(2)}, u32[]{:S(2)}) %all-to-all-start.3) | async-done | bytes 1835040 | tf_op jit(solution)/shard_map/all_to_all | solution.py:34
  472.2 2.7 reduce_sum.42
  (3 shorter events, 0.1 us)
Async XLA Ops:
  7.2 415.1 %copy-start = (bf16[128,7168]{1,0:T(8,128)(2,1)S(1)}, bf16[128,7168]{1,0:T(8,128)(2,1)}, u32[]{:S(2)}) copy-start(bf16[128,7168]{1,0:T(8,128)(2,1)} %param.6) | copy-start | bytes 5505028
  7.2 137.3 %all-gather.2.cloned.1.call-start = ((), (), s32[]{:S(2)}) async-start(), calls=%async_computation.4 | async-start | bytes 20680704 | tf_op jit(solution)/shard_map/all_gather | solution.py:61
  9.9 157.4 %copy-start.1 = (bf16[224,384]{1,0:T(8,128)(2,1)S(1)}, bf16[224,384]{1,0:T(8,128)(2,1)}, u32[]{:S(2)}) copy-start(bf16[224,384]{1,0:T(8,128)(2,1)} %param.7) | copy-start | bytes 516100
  170.2 252.0 %copy-start.2 = (f32[384]{0:T(512)S(1)}, f32[384]{0:T(512)}, u32[]{:S(2)}) copy-start(f32[384]{0:T(512)} %param.8) | copy-start | bytes 4612
  170.2 252.0 %all-to-all-start = ((bf16[32,224,384]{2,1,0:T(8,128)(2,1)}), bf16[32,224,384]{2,1,0:T(8,128)(2,1)}, u32[]{:S(2)}, u32[]{:S(2)}) async-start(bf16[32,224,384]{2,1,0:T(8,128)(2,1)} %stack.2), calls=%async_computation | async-start | bytes 11010048 | tf_op jit(solution)/shard_map/all_to_all | solution.py:53
  436.0 10.8 %all-to-all-start.1 = ((bf16[4,128,384]{1,2,0:T(8,128)(2,1)}), bf16[4,128,384]{1,2,0:T(8,128)(2,1)S(1)}, u32[]{:S(2)}, u32[]{:S(2)}) async-start(bf16[4,128,384]{1,2,0:T(8,128)(2,1)} %broadcast_in_dim.7), calls=%async_computation.1 | async-start | bytes 786432 | tf_op jit(solution)/shard_map/all_to_all | solution.py:17
  446.9 25.3 %all-to-all-start.3 = ((bf16[4,128,1792]{2,1,0:T(8,128)(2,1)}), bf16[4,128,1792]{2,1,0:T(8,128)(2,1)}, u32[]{:S(2)}, u32[]{:S(2)}) async-start(bf16[4,128,1792]{2,1,0:T(8,128)(2,1)} %bitcast.30), calls=%async_computation.3 | async-start | bytes 3670016 | tf_op jit(solution)/shard_map/all_to_all | solution.py:34
Sparse Core Ops, SparseCore 0:
  9.9 134.5 all-gather.1
